TPU v7x, 128 devices: a whole 4x4x4 slice. The times are simulated.
128 devices in a mesh: row: 64 (over y, x, z_hi, core), col: 2 (over z_lo).
Axes of the slice: x: 4, y: 4, z: 4 (z_hi: 2, z_lo: 2; z = z_hi * 2 + z_lo), core: 2. Of those that a mesh axis runs over, the one named last changes fastest.
Arguments:
- tokens: bfloat16 [1024, 8192], P('row', 'col'), may hold values from -6 to 6
- norm_gain: float32 [8192], P('col'), may hold values from 0.1 to 1.9
- gate_weight: bfloat16 [8192, 28672], P('col', 'row'), may hold values from -0.0625 to 0.0625
- up_weight: bfloat16 [8192, 28672], P('col', 'row'), may hold values from -0.0625 to 0.0625
- down_weight: bfloat16 [28672, 8192], P('row', 'col'), may hold values from -0.03125 to 0.03125
Outputs:
- mixed: bfloat16 [1024, 8192], P('row', 'col')
All inputs are finite; a program needn't handle non-finite values.
Results may differ from a plain program's by a relative error of at most 0.0065.
Values may be sent and summed in bfloat16 or wider, within the bound.
A program may use at most 128 MiB of HBM per device.

v0:
```python
import jax
import jax.numpy as jnp
from jax import lax
from jax.sharding import Mesh
from jax.sharding import PartitionSpec as P

D = 8192
ROW = ("row_0", "row_1", "row_2", "row_3")


def copy_for_each(x, axis):
    copies = jnp.broadcast_to(x, (lax.axis_size(axis), *x.shape))
    return lax.all_to_all(copies, axis, split_axis=0, concat_axis=0, tiled=True)


def taken_together(x, axis):
    everything = copy_for_each(x, axis)
    return jnp.sum(everything, axis=0)


def in_blocks(x, dim, count):
    before, after = (x.shape[:dim], x.shape[dim + 1 :])
    return jnp.moveaxis(x.reshape(*before, count, -1, *after), dim, 0)


def sum_at_owner(x, axis, dim):
    count = lax.axis_size(axis)
    blocks = lax.all_to_all(in_blocks(x, dim, count), axis, 0, 0, tiled=True)
    return jnp.sum(blocks, axis=0)


def in_order(blocks, dim):
    blocks = jnp.moveaxis(blocks, 0, dim)
    dims = blocks.shape
    return blocks.reshape(*dims[:dim], dims[dim] * dims[dim + 1], *dims[dim + 2 :])


def collect(x, axis, dim):
    blocks = copy_for_each(x, axis)
    return in_order(blocks, dim)


def summed_rows(x, chips, core, dim):
    sizes = (lax.axis_size(chips), lax.axis_size(core))
    blocks = in_blocks(x, dim, sizes[0] * sizes[1])
    inside = blocks.shape[1:]
    blocks = blocks.reshape(*sizes, *inside).swapaxes(0, 1).reshape(-1, *inside)
    blocks = lax.psum_scatter(blocks, core, scatter_dimension=0, tiled=True)
    return lax.psum_scatter(blocks, chips, scatter_dimension=0, tiled=True)[0]


def gated(both, width):
    return (jax.nn.silu(both[:, :width]) * both[:, width:]).astype(jnp.bfloat16)


def on_device(tokens, norm_gain, gate_weight, up_weight, down_weight):
    widened = tokens.astype(jnp.float32)
    squares = taken_together(jnp.sum(widened * widened, axis=1, keepdims=True), "col")
    normed = (widened * norm_gain[None, :] / jnp.sqrt(squares / D + 1e-05)).astype(jnp.bfloat16)
    width = gate_weight.shape[1]
    piece = lax.all_gather(normed, ROW, axis=0, tiled=True)
    gate_part = jnp.dot(piece, gate_weight, preferred_element_type=jnp.float32)
    up_part = jnp.dot(piece, up_weight, preferred_element_type=jnp.float32)
    partial_value = jnp.concatenate([gate_part, up_part], axis=1)
    shares = sum_at_owner(partial_value, "col", 0)
    hidden = collect(gated(shares, width), "col", 0)
    mixed = summed_rows(
        jnp.dot(hidden, down_weight, preferred_element_type=jnp.float32),
        ("row_0", "row_1", "row_2"),
        "row_3",
        0,
    )
    return mixed.astype(jnp.bfloat16)


def solution(mesh):
    finer = Mesh(
        mesh.devices.reshape(4, 4, 2, 2, mesh.shape["col"]),
        ("row_0", "row_1", "row_2", "row_3", "col"),
    )
    placed = (P(ROW, "col"), P("col"), P("col", ROW), P("col", ROW), P(ROW, "col"))
    return jax.shard_map(
        on_device, mesh=finer, in_specs=placed, out_specs=P(ROW, "col"), check_vma=False
    )
```

profile of v0, /device:TPU:0, one launch (start us, length us, event | category | flops | bytes accessed | tf_op | source)
XLA Modules:
  0.0 435.2 jit_solution(14296491897519222040)
XLA Ops:
  6.5 0.0 all-gather.2.cloned.1.call-start
  6.5 1.0 fusion.4
  7.6 6.9 %all_to_all.15 = f32[2,16,1]{1,2,0:T(1,128)S(1)} all-to-all(f32[2,16,1]{1,2,0:T(1,128)S(1)} %broadcast_in_dim.8), channel_id=1, replica_groups=mesh['row_0'=4,'row_1'=4,'row_2'=2,'row_3'=2,'col'=2] {'col'}, dimensions={0} | all-to-all | bytes 256 | tf_op jit(solution)/shard_map/all_to_all | solution.py:13
  14.5 1.7 fusion.3
  16.2 0.0 all-gather.2.cloned.1.call-update
  16.2 0.0 reduce-scatter.3.cloned.1.call-start
  16.2 85.4 %all-gather.2.cloned.1.call-done = bf16[1024,4096]{1,0:T(8,128)(2,1)} async-done(((bf16[16,4096]{1,0:T(8,128)(2,1)}), bf16[1024,4096]{1,0:T(8,128)(2,1)}) %all-gather.2.cloned.1.call-update) | async-done | bytes 8388624 | tf_op jit(solution)/shard_map/all_gather | solution.py:61
  101.6 0.0 copy-start
  101.6 0.0 copy-start.1
  101.6 7.7 %fusion.6 = f32[1024,448]{0,1:T(8,128)S(1)} fusion(bf16[1024,4096]{1,0:T(8,128)(2,1)} %all-gather.2.cloned.1.call-done, bf16[4096,448]{0,1:T(8,128)(2,1)} %param.8), kind=kOutput, calls=%fused_computation.14 | convolution fusion | flops 3758096384 | bytes 13893632 | tf_op jit(solution)/shard_map/dot_general | solution.py:63
  109.3 0.0 copy-done
  109.3 0.2 copy-done.1
  109.5 4.0 fusion.5
  113.5 0.5 pad_maximum_fusion
  114.0 0.5 copy.17
  114.5 46.0 %all_to_all.16 = f32[2,512,896]{1,2,0:T(8,128)} all-to-all(f32[2,512,896]{1,2,0:T(8,128)S(1)} %bitcast.22), channel_id=1, replica_groups=mesh['row_0'=4,'row_1'=4,'row_2'=2,'row_3'=2,'col'=2] {'col'}, dimensions={0} | all-to-all | bytes 7340032 | tf_op jit(solution)/shard_map/all_to_all | solution.py:28
  160.5 2.6 reduce_sum.29
  163.1 0.3 fusion.1
  163.4 0.1 broadcast_in_dim.9
  163.5 14.5 %all_to_all.17 = bf16[2,512,448]{1,2,0:T(8,128)(2,1)S(1)} all-to-all(bf16[2,512,448]{1,2,0:T(8,128)(2,1)S(1)} %broadcast_in_dim.9), channel_id=1, replica_groups=mesh['row_0'=4,'row_1'=4,'row_2'=2,'row_3'=2,'col'=2] {'col'}, dimensions={0} | all-to-all | bytes 1835008 | tf_op jit(solution)/shard_map/all_to_all | solution.py:13
  177.9 0.5 copy.9
  178.4 6.6 %convolution_bitcast_fusion = f32[2,32,16,4096]{3,2,0,1:T(8,128)S(1)} fusion(bf16[32,2,16,448]{3,2,1,0:T(8,128)(2,1)S(1)} %bitcast.23, bf16[448,4096]{1,0:T(8,128)(2,1)} %param.9), kind=kOutput, calls=%fused_computation | convolution fusion | flops 3758096384 | bytes 21364736 | tf_op jit(solution)/shard_map/dot_general | solution.py:68
  185.0 6.0 %copy.10 = f32[2,32,16,4096]{3,2,1,0:T(8,128)} copy(f32[2,32,16,4096]{3,2,0,1:T(8,128)S(1)} %convolution_bitcast_fusion) | data formatting | bytes 33554432 | tf_op jit(solution)/shard_map/transpose | solution.py:47
  191.0 0.0 reduce-scatter.3.cloned.1.call-update
  191.0 0.0 reduce-scatter.5.cloned.1.call-start
  191.1 24.7 %reduce-scatter.3.cloned.1.call-done = f32[32,16,4096]{2,1,0:T(8,128)} async-done(((f32[64,16,4096]{2,1,0:T(8,128)}), f32[32,16,4096]{2,1,0:T(8,128)}) %reduce-scatter.3.cloned.1.call-update) | async-done | bytes 8388624 | tf_op jit(solution)/shard_map/reduce_scatter | solution.py:48
  215.8 0.0 reduce-scatter.5.cloned.1.call-update
  215.8 211.3 %reduce-scatter.5.cloned.1.call-done = f32[1,16,4096]{2,1,0:T(8,128)} async-done(((f32[32,16,4096]{2,1,0:T(8,128)}), f32[1,16,4096]{2,1,0:T(8,128)}) %reduce-scatter.5.cloned.1.call-update) | async-done | bytes 262160 | tf_op jit(solution)/shard_map/reduce_scatter | solution.py:49
  427.0 1.6 convert_bitcast_fusion
  (3 shorter events, 0.0 us)
Async XLA Ops:
  6.5 95.1 %all-gather.2.cloned.1.call-start = ((), (), s32[]{:S(2)}) async-start(), calls=%async_computation.5 | async-start | bytes 8519680 | tf_op jit(solution)/shard_map/all_gather | solution.py:61
  16.2 199.6 %reduce-scatter.3.cloned.1.call-start = ((), (), s32[]{:S(2)}) async-start(), calls=%async_computation.6 | async-start | bytes 25165824 | tf_op jit(solution)/shard_map/reduce_scatter | solution.py:48
  101.6 7.7 %copy-start = (bf16[1024,4096]{1,0:T(8,128)(2,1)S(1)}, bf16[1024,4096]{1,0:T(8,128)(2,1)}, u32[]{:S(2)}) copy-start(bf16[1024,4096]{1,0:T(8,128)(2,1)} %all-gather.2.cloned.1.call-done) | copy-start | bytes 25165828
  101.6 7.9 %copy-start.1 = (bf16[4096,448]{0,1:T(8,128)(2,1)S(1)}, bf16[4096,448]{0,1:T(8,128)(2,1)}, u32[]{:S(2)}) copy-start(bf16[4096,448]{0,1:T(8,128)(2,1)} %param.7) | copy-start | bytes 11010052
  191.0 236.0 %reduce-scatter.5.cloned.1.call-start = ((), (), s32[]{:S(2)}) async-start(), calls=%async_computation.7 | async-start | bytes 8650752 | tf_op jit(solution)/shard_map/reduce_scatter | solution.py:49
Sparse Core Ops, SparseCore 0:
  16.3 85.2 all-gather.1
  191.2 24.5 reduce-scatter.2
  218.2 208.8 reduce-scatter.4
where the time goes:
time: 436 us; the launch traced here: 435 us
  waiting for transfers between devices  321 us (74%)
  blocking collectives  67.4 us (15%)
  matrix products  18.2 us (4%)
  between operations  13.2 us (3%)
  other arithmetic  7.72 us (2%)
  local copies, waits for them, and re-layouts  7.32 us (2%)
    reduce_scatter x1, waiting for transfers between devices, summed_rows(): return lax.psum_scatter(blocks, chips, scatter_dimension=0, tiled=True)[0]  211 us
    all_gather x1, waiting for transfers between devices, on_device(): piece = lax.all_gather(normed, ROW, axis=0, tiled=True)  85.4 us
    all_to_all x1, blocking collectives, sum_at_owner(): blocks = lax.all_to_all(in_blocks(x, dim, count), axis, 0, 0, tiled=True)  46 us
    reduce_scatter x1, waiting for transfers between devices, summed_rows(): blocks = lax.psum_scatter(blocks, core, scatter_dimension=0, tiled=True)  24.7 us
    all_to_all x2, blocking collectives, copy_for_each(): return lax.all_to_all(copies, axis, split_axis=0, concat_axis=0, tiled=True)  21.3 us
  transfers between devices with their start and end apart: 3, of which 3 were waited for; matrix products, arithmetic and copies ran while one was open for 0% of the time, Pallas kernels for 0%

commit v1 on v0

--- a/solution.py
+++ b/solution.py
@@ -58,7 +58,8 @@
     squares = taken_together(jnp.sum(widened * widened, axis=1, keepdims=True), "col")
     normed = (widened * norm_gain[None, :] / jnp.sqrt(squares / D + 1e-05)).astype(jnp.bfloat16)
     width = gate_weight.shape[1]
-    piece = lax.all_gather(normed, ROW, axis=0, tiled=True)
+    outgoing = jnp.stack([normed] * lax.axis_size(ROW))
+    piece = jnp.concatenate(lax.all_to_all(outgoing, ROW, 0, 0), axis=0)
     gate_part = jnp.dot(piece, gate_weight, preferred_element_type=jnp.float32)
     up_part = jnp.dot(piece, up_weight, preferred_element_type=jnp.float32)
     partial_value = jnp.concatenate([gate_part, up_part], axis=1)

time: 436 us -> 456 us (1.046)
  blocking collectives: 67.4 us -> 176 us
  waiting for transfers between devices: 321 us -> 236 us
    all_to_all x0 -> x1, blocking collectives: none -> 109 us  [on_device(): piece = jnp.concatenate(lax.all_to_all(outgoing, ROW, 0, 0), axis=0)]
    all_gather x1 -> x0, waiting for transfers between devices: 85.4 us -> none  [on_device(): piece = lax.all_gather(normed, ROW, axis=0, tiled=True)]
  transfers between devices with their start and end apart: 3 -> 2, of which waited for: 3 -> 2; matrix products, arithmetic and copies ran while one was open for 0% -> 0% of each run, Pallas kernels for 0% -> 0%
where the time goes in v1:
time: 456 us; the launch traced here: 455 us
  waiting for transfers between devices  236 us (52%)
  blocking collectives  176 us (39%)
  matrix products  14.5 us (3%)
  between operations  13.5 us (3%)
  local copies, waits for them, and re-layouts  8.11 us (2%)
  other arithmetic  7.06 us (2%)
    reduce_scatter x1, waiting for transfers between devices, summed_rows(): return lax.psum_scatter(blocks, chips, scatter_dimension=0, tiled=True)[0]  211 us
    all_to_all x1, blocking collectives, on_device(): piece = jnp.concatenate(lax.all_to_all(outgoing, ROW, 0, 0), axis=0)  109 us
    all_to_all x1, blocking collectives, sum_at_owner(): blocks = lax.all_to_all(in_blocks(x, dim, count), axis, 0, 0, tiled=True)  46 us
    reduce_scatter x1, waiting for transfers between devices, summed_rows(): blocks = lax.psum_scatter(blocks, core, scatter_dimension=0, tiled=True)  24.4 us
    all_to_all x2, blocking collectives, copy_for_each(): return lax.all_to_all(copies, axis, split_axis=0, concat_axis=0, tiled=True)  21.3 us
  transfers between devices with their start and end apart: 2, of which 2 were waited for; matrix products, arithmetic and copies ran while one was open for 0% of the time, Pallas kernels for 0%

profile of v1, /device:TPU:0, one launch (start us, length us, event | category | flops | bytes accessed | tf_op | source)
XLA Modules:
  0.0 455.2 jit_solution(8718932914547556747)
XLA Ops:
  6.5 0.0 reduce-scatter.3.cloned.1.call-start
  6.5 1.0 fusion.4
  7.6 6.9 %all_to_all.20 = f32[2,16,1]{1,2,0:T(1,128)S(1)} all-to-all(f32[2,16,1]{1,2,0:T(1,128)S(1)} %broadcast_in_dim.8), channel_id=1, replica_groups=mesh['row_0'=4,'row_1'=4,'row_2'=2,'row_3'=2,'col'=2] {'col'}, dimensions={0} | all-to-all | bytes 256 | tf_op jit(solution)/shard_map/all_to_all | solution.py:13
  14.5 1.0 fusion.3
  15.5 1.0 stack.2
  16.5 0.0 copy-start
  16.6 108.7 %all_to_all.21 = bf16[64,16,4096]{2,1,0:T(8,128)(2,1)S(1)} all-to-all(bf16[64,16,4096]{2,1,0:T(8,128)(2,1)S(1)} %stack.2), channel_id=1, replica_groups=mesh['row_0'=4,'row_1'=4,'row_2'=2,'row_3'=2,'col'=2] {'row_0','row_1','..., dimensions={0} | all-to-all | bytes 16777216 | tf_op jit(solution)/shard_map/all_to_all | solution.py:62
  125.3 0.0 copy-done
  125.3 0.0 copy-start.1
  125.3 4.0 fusion.6
  129.3 0.0 copy-done.1
  129.3 4.0 fusion.5
  133.3 0.5 pad_maximum_fusion
  133.8 0.5 copy.17
  134.2 46.0 %all_to_all.22 = f32[2,512,896]{1,2,0:T(8,128)} all-to-all(f32[2,512,896]{1,2,0:T(8,128)S(1)} %bitcast.23), channel_id=1, replica_groups=mesh['row_0'=4,'row_1'=4,'row_2'=2,'row_3'=2,'col'=2] {'col'}, dimensions={0} | all-to-all | bytes 7340032 | tf_op jit(solution)/shard_map/all_to_all | solution.py:28
  180.3 2.6 reduce_sum.29
  182.9 0.3 fusion.1
  183.2 0.1 broadcast_in_dim.9
  183.2 14.4 %all_to_all.23 = bf16[2,512,448]{1,2,0:T(8,128)(2,1)S(1)} all-to-all(bf16[2,512,448]{1,2,0:T(8,128)(2,1)S(1)} %broadcast_in_dim.9), channel_id=1, replica_groups=mesh['row_0'=4,'row_1'=4,'row_2'=2,'row_3'=2,'col'=2] {'col'}, dimensions={0} | all-to-all | bytes 1835008 | tf_op jit(solution)/shard_map/all_to_all | solution.py:13
  197.7 0.5 copy.9
  198.2 6.6 %convolution_bitcast_fusion = f32[2,32,16,4096]{3,2,0,1:T(8,128)S(1)} fusion(bf16[32,2,16,448]{3,2,1,0:T(8,128)(2,1)S(1)} %bitcast.26, bf16[448,4096]{1,0:T(8,128)(2,1)} %param.9), kind=kOutput, calls=%fused_computation | convolution fusion | flops 3758096384 | bytes 21364736 | tf_op jit(solution)/shard_map/dot_general | solution.py:69
  204.8 6.0 %copy.10 = f32[2,32,16,4096]{3,2,1,0:T(8,128)} copy(f32[2,32,16,4096]{3,2,0,1:T(8,128)S(1)} %convolution_bitcast_fusion) | data formatting | bytes 33554432 | tf_op jit(solution)/shard_map/transpose | solution.py:47
  210.8 0.0 reduce-scatter.3.cloned.1.call-update
  210.8 0.0 reduce-scatter.5.cloned.1.call-start
  210.9 24.4 %reduce-scatter.3.cloned.1.call-done = f32[32,16,4096]{2,1,0:T(8,128)} async-done(((f32[64,16,4096]{2,1,0:T(8,128)}), f32[32,16,4096]{2,1,0:T(8,128)}) %reduce-scatter.3.cloned.1.call-update) | async-done | bytes 8388624 | tf_op jit(solution)/shard_map/reduce_scatter | solution.py:48
  235.2 0.0 reduce-scatter.5.cloned.1.call-update
  235.2 211.4 %reduce-scatter.5.cloned.1.call-done = f32[1,16,4096]{2,1,0:T(8,128)} async-done(((f32[32,16,4096]{2,1,0:T(8,128)}), f32[1,16,4096]{2,1,0:T(8,128)}) %reduce-scatter.5.cloned.1.call-update) | async-done | bytes 262160 | tf_op jit(solution)/shard_map/reduce_scatter | solution.py:49
  446.7 1.6 convert_bitcast_fusion
  (3 shorter events, 0.0 us)
Async XLA Ops:
  6.5 228.7 %reduce-scatter.3.cloned.1.call-start = ((), (), s32[]{:S(2)}) async-start(), calls=%async_computation.6 | async-start | bytes 25165824 | tf_op jit(solution)/shard_map/reduce_scatter | solution.py:48
  16.5 108.8 %copy-start = (bf16[4096,448]{0,1:T(8,128)(2,1)S(1)}, bf16[4096,448]{0,1:T(8,128)(2,1)}, u32[]{:S(2)}) copy-start(bf16[4096,448]{0,1:T(8,128)(2,1)} %param.8) | copy-start | bytes 11010052
  125.3 4.0 copy-start.1
  210.8 235.9 %reduce-scatter.5.cloned.1.call-start = ((), (), s32[]{:S(2)}) async-start(), calls=%async_computation.7 | async-start | bytes 8650752 | tf_op jit(solution)/shard_map/reduce_scatter | solution.py:49
Sparse Core Ops, SparseCore 0:
  210.9 24.2 reduce-scatter.2
  237.6 209.0 reduce-scatter.4
